TPU v7x, 32 devices: a whole 2x2x4 slice. The times are simulated.
32 devices in a mesh: rows: 8 (over z, y), grp: 4 (over x, core).
Axes of the slice: x: 2, y: 2, z: 4, core: 2. Of those that a mesh axis runs over, the one named last changes fastest.
Arguments:
- modes: float32 [393216, 256], P(('rows', 'grp')), may hold values from -6 to 6
- points: int32 [196], replicated, may hold values from 0 to 393215, as said below
Outputs:
- residual: float32 [393216, 128], P(('rows', 'grp'))
- norms: float32 [4, 128], replicated
Inputs may be any that keep to these rules, and one draw needn't show every extreme that they name: `points`: distinct row indices of the mode matrix.
All inputs are finite; a program needn't handle non-finite values.
Results may differ from a plain program's by a relative error of at most 0.00029.
Values sent between devices are 32-bit elements; how exact they have to be, the bound alone decides.
A program may use at most 128 MiB of HBM per device.

v0:
```python
import jax
import jax.numpy as jnp
from jax import lax
from jax.sharding import PartitionSpec as P

FIT = 128
PRIOR = 192
STEPS = 4


def outer_add(gram, cross, fresh, split):
    left = fresh[:split]
    right = fresh[split:]
    return (gram + left[:, None] * left[None, :], cross + left[:, None] * right[None, :])


def on_device(modes, points):
    high = lax.Precision.HIGHEST
    rows_dev = modes.shape[0]
    split = FIT
    total = rows_dev * lax.axis_size(("rows", "grp"))
    base = lax.axis_index(("rows", "grp")) * rows_dev
    local_idx = points - base
    owned = (local_idx >= 0) & (local_idx < rows_dev)
    safe_idx = jnp.clip(local_idx, 0, rows_dev - 1)
    picked = jnp.where(owned[:, None], modes[safe_idx], 0.0)
    fit_modes = modes[:, :split]
    rest_modes = modes[:, split:]
    prior_count = PRIOR
    local_ftf = jnp.dot(fit_modes.T, fit_modes, preferred_element_type=jnp.float32, precision=high)
    local_ftr = jnp.dot(fit_modes.T, rest_modes, preferred_element_type=jnp.float32, precision=high)
    local_sq = jnp.sum(rest_modes * rest_modes, axis=0)
    block, ftf, ftr, sq_total = lax.psum((picked, local_ftf, local_ftr, local_sq), ("rows", "grp"))
    left = block[:prior_count, :split]
    gram = jnp.dot(left.T, left, preferred_element_type=jnp.float32, precision=high)
    cross = jnp.dot(
        left.T, block[:prior_count, split:], preferred_element_type=jnp.float32, precision=high
    )
    new_rows = block[prior_count:]
    collected = []
    coef = cross
    for step in range(STEPS):
        gram, cross = outer_add(gram, cross, new_rows[step], split)
        factor = jnp.linalg.cholesky(gram)
        coef = jax.scipy.linalg.cho_solve((factor, True), cross)
        curved = jnp.dot(ftf, coef, preferred_element_type=jnp.float32, precision=high)
        summed = sq_total - 2.0 * jnp.sum(coef * ftr, axis=0) + jnp.sum(coef * curved, axis=0)
        collected.append(summed / total)
    residual = rest_modes - jnp.dot(
        fit_modes, coef, preferred_element_type=jnp.float32, precision=high
    )
    return (residual, jnp.stack(collected))


def solution(mesh):
    return jax.shard_map(
        on_device,
        mesh=mesh,
        in_specs=(P(("rows", "grp"), None), P()),
        out_specs=(P(("rows", "grp"), None), P()),
        check_vma=False,
    )
```

profile of v0, /device:TPU:0, one launch (start us, length us, event | category | flops | bytes accessed | tf_op | source)
XLA Modules:
  0.0 294.0 jit_solution(1023648087928314407)
XLA Ops:
  7.2 0.7 compare_and_fusion
  7.9 0.7 compare_select_fusion
  8.6 14.0 %fusion.3 = f32[128,128]{1,0:T(8,128)} fusion(f32[12288,256]{1,0:T(8,128)} %param.5), kind=kOutput, calls=%fused_computation.6 | convolution fusion | flops 2415919104 | bytes 12648448 | tf_op jit(solution)/shard_map/dot_general | solution.py:31
  22.6 10.7 %fusion.1 = f32[128,128]{1,0:T(8,128)} fusion(f32[12288,256]{1,0:T(8,128)S(1)} %copy-done), kind=kOutput, calls=%fused_computation.4 | convolution fusion | flops 2415919104 | bytes 6356992 | tf_op jit(solution)/shard_map/dot_general | solution.py:30
  33.2 5.4 %gather_fusion = f32[196,256]{1,0:T(8,128)S(1)} fusion(f32[12288,256]{1,0:T(8,128)} %param.5, s32[1024]{0:T(1024)S(1)} %pad_clamp_fusion), kind=kCustom, calls=%fused_computation | custom fusion | bytes 402192 | tf_op jit(solution)/shard_map/gather | solution.py:26
  38.7 0.8 broadcast_select_fusion
  39.5 4.8 %slice.73 = f32[12288,128]{1,0:T(8,128)} slice(f32[12288,256]{1,0:T(8,128)} %param.5), slice={[0:12288], [128:256]} | slice | bytes 12582912
  44.3 6.6 %copy.14 = f32[12288,128]{0,1:T(8,128)} copy(f32[12288,128]{1,0:T(8,128)} %slice.73) | data formatting | bytes 12582912
  50.9 3.3 %multiply_reduce_fusion = f32[128]{0:T(128)S(1)} fusion(f32[12288,128]{0,1:T(8,128)} %copy.14), kind=kLoop, calls=%fused_computation.3 | loop fusion | flops 3145600 | bytes 6291968 | tf_op jit(solution)/shard_map/reduce_sum | solution.py:32
  54.2 42.2 %psum.29 = f32[128]{0:T(128)S(1)} all-reduce(f32[128]{0:T(128)S(1)} %multiply_reduce_fusion), channel_id=1, replica_groups=mesh['rows'=8,'grp'=4] {'rows','grp'}, use_global_device_ids=true, to_apply=%region_4.0 | all-reduce | flops 128 | bytes 1024 | tf_op jit(solution)/shard_map/psum | solution.py:33
  96.3 74.0 %all-reduce.3.cloned.1.call-done = (f32[196,256]{1,0:T(8,128)}, f32[128,128]{1,0:T(8,128)}, f32[128,128]{1,0:T(8,128)}) async-done(((f32[196,256]{1,0:T(8,128)}, f32[128,128]{1,0:T(8,128)}, f32[128,128]{1,0:T(8,128)}), (f32[196,256]{1,0:T(8,128)}, f32[128,128]{1,0:T(8,128)}, f32[128,128]{1,0:T(8,128)})) %all-reduce.3.cloned.1.call-update) | async-done | bytes 331792 | tf_op jit(solution)/shard_map/psum | solution.py:33
  170.3 0.8 slice_bitcast_fusion.2
  171.2 1.4 convolution_add_fusion
  172.5 1.4 multiply_add_fusion.2
  174.3 11.7 %cholesky.107 = f32[128,128]{1,0:T(8,128)S(1)} custom-call(f32[128,128]{1,0:T(8,128)S(1)} %get-tuple-element.30), custom_call_target="Cholesky" | custom-call | tf_op jit(solution)/shard_map/jit(cholesky)/cholesky | solution.py:44
  187.3 9.8 %custom-call.13 = f32[1,128,128]{1,2,0:T(8,128)S(1)} custom-call(f32[1,128,128]{2,1,0:T(8,128)S(1)} %fusion.16), custom_call_target="InvertDiagBlocksLowerTriangular" | custom-call | tf_op jit(solution)/shard_map/jit(_cho_solve)/triangular_solve | solution.py:45
  197.1 11.7 %cholesky.96 = f32[128,128]{1,0:T(8,128)S(1)} custom-call(f32[128,128]{1,0:T(8,128)S(1)} %get-tuple-element.31), custom_call_target="Cholesky" | custom-call | tf_op jit(solution)/shard_map/jit(cholesky)/cholesky | solution.py:44
  210.2 10.2 %custom-call.12 = f32[1,128,128]{1,2,0:T(8,128)S(1)} custom-call(f32[1,128,128]{2,1,0:T(8,128)S(1)} %fusion.15), custom_call_target="InvertDiagBlocksLowerTriangular" | custom-call | tf_op jit(solution)/shard_map/jit(_cho_solve)/triangular_solve | solution.py:45
  221.1 11.7 %cholesky.74 = f32[128,128]{1,0:T(8,128)S(1)} custom-call(f32[128,128]{1,0:T(8,128)S(1)} %get-tuple-element.33), custom_call_target="Cholesky" | custom-call | tf_op jit(solution)/shard_map/jit(cholesky)/cholesky | solution.py:44
  234.1 9.8 %custom-call.10 = f32[1,128,128]{1,2,0:T(8,128)S(1)} custom-call(f32[1,128,128]{2,1,0:T(8,128)S(1)} %fusion.13), custom_call_target="InvertDiagBlocksLowerTriangular" | custom-call | tf_op jit(solution)/shard_map/jit(_cho_solve)/triangular_solve | solution.py:45
  244.5 10.5 %fusion = f32[12288,128]{0,1:T(8,128)} fusion(f32[12288,128]{0,1:T(8,128)} %copy.14, f32[128,128]{1,0:T(8,128)S(1)} %fusion.32, f32[12288,256]{1,0:T(8,128)} %param.5), kind=kOutput, calls=%fused_computation.2 | convolution fusion | flops 2417491968 | bytes 18939904 | tf_op jit(solution)/shard_map/dot_general | solution.py:49
  256.2 11.7 %cholesky.85 = f32[128,128]{1,0:T(8,128)S(1)} custom-call(f32[128,128]{1,0:T(8,128)S(1)} %get-tuple-element.32), custom_call_target="Cholesky" | custom-call | tf_op jit(solution)/shard_map/jit(cholesky)/cholesky | solution.py:44
  269.3 9.8 %custom-call.11 = f32[1,128,128]{1,2,0:T(8,128)S(1)} custom-call(f32[1,128,128]{2,1,0:T(8,128)S(1)} %fusion.14), custom_call_target="InvertDiagBlocksLowerTriangular" | custom-call | tf_op jit(solution)/shard_map/jit(_cho_solve)/triangular_solve | solution.py:45
  279.9 6.6 %copy.11 = f32[12288,128]{1,0:T(8,128)} copy(f32[12288,128]{0,1:T(8,128)} %fusion) | data formatting | bytes 12582912
  (41 shorter events, 9.4 us)
Async XLA Ops:
  7.2 163.2 %all-reduce.3.cloned.1.call-start = ((), (), s32[]{:S(2)}) async-start(), calls=%async_computation | async-start | bytes 671744 | tf_op jit(solution)/shard_map/psum | solution.py:33
  8.6 14.0 %copy-start = (f32[12288,256]{1,0:T(8,128)S(1)}, f32[12288,256]{1,0:T(8,128)}, u32[]{:S(2)}) copy-start(f32[12288,256]{1,0:T(8,128)} %param.5) | copy-start | bytes 37748740
  244.5 10.5 %copy-start.1 = (f32[128,128]{1,0:T(8,128)S(1)}, f32[128,128]{1,0:T(8,128)}, u32[]{:S(2)}) copy-start(f32[128,128]{1,0:T(8,128)} %get-tuple-element.11) | copy-start | bytes 196612
  244.5 34.9 %copy-start.2 = (f32[128,128]{1,0:T(8,128)S(1)}, f32[128,128]{1,0:T(8,128)}, u32[]{:S(2)}) copy-start(f32[128,128]{1,0:T(8,128)} %get-tuple-element.12) | copy-start | bytes 196612
Sparse Core Ops, SparseCore 0:
  39.6 130.6 all-reduce.2
where the time goes:
time: 299 us; the launch traced here: 294 us
  other arithmetic  97.9 us (33%)
  waiting for transfers between devices  74 us (25%)
  blocking collectives  42.2 us (14%)
  matrix products  40.9 us (14%)
  local copies, waits for them, and re-layouts  24.6 us (8%)
  between operations  14.5 us (5%)
    psum x1, waiting for transfers between devices, on_device(): lax.psum((picked, local_ftf, local_ftr, local_sq), ('rows', 'grp'))  74 us
    another operation x12, other arithmetic, on_device(): factor = jnp.linalg.cholesky(gram)  49.6 us
    another operation x8, other arithmetic, on_device(): coef = jax.scipy.linalg.cho_solve((factor, True), cross)  42.3 us
    psum x1, blocking collectives, on_device(): lax.psum((picked, local_ftf, local_ftr, local_sq), ('rows', 'grp'))  42.2 us
    unnamed x9, local copies, waits for them, and re-layouts  18 us
    dot_general x1, matrix products, on_device(): jnp.dot(fit_modes.T, rest_modes, preferred_element_type=jnp.float32, prec...  14 us
    dot_general x1, matrix products, on_device(): jnp.dot(fit_modes.T, fit_modes, preferred_element_type=jnp.float32, preci...  10.7 us
    dot_general x1, matrix products, on_device(): jnp.dot(fit_modes, coef, preferred_element_type=jnp.float32, precision=high)  10.5 us
  transfers between devices with their start and end apart: 1, of which 1 were waited for; matrix products, arithmetic and copies ran while one was open for 5% of the time, Pallas kernels for 0%

commit v1 on v0

v1 whole, which is shorter than its diff:
```python
import functools

import jax
import jax.numpy as jnp
from jax import lax
from jax.experimental import pallas as pl
from jax.experimental.pallas import tpu as pltpu
from jax.sharding import PartitionSpec as P

PRIOR = 192
LANES = 128
HIGH = lax.Precision.HIGHEST
MESH = pl.DeviceIdType.MESH


def dot(a, b, dims=((1,), (0,))):
    return lax.dot_general(a, b, (dims, ((), ())), precision=HIGH, preferred_element_type=jnp.float32)


def flat_index(axes):
    (first, _), (second, width) = axes
    return lax.axis_index(first) * width + lax.axis_index(second)


def coords(axes, flat):
    width = axes[1][1]
    return (flat // width, lax.rem(flat, width))


def pick_kernel(axes, n, points_ref, modes_ref, out_ref, picked, sem):
    rows_dev, cols = modes_ref.shape
    npts = points_ref.shape[0]
    split = cols // 2
    base = flat_index(axes) * rows_dev
    picked[...] = jnp.zeros_like(picked)

    def row_copy(i):
        local = points_ref[i] - base
        owned = (local >= 0) & (local < rows_dev)
        safe = jnp.clip(local, 0, rows_dev - 1)
        return owned, pltpu.make_async_copy(
            modes_ref.at[pl.ds(safe, 1), :], picked.at[pl.ds(i, 1), :], sem
        )

    def issue(i, count):
        owned, copy = row_copy(i)

        @pl.when(owned)
        def _():
            copy.start()

        return count

    def drain(i, count):
        owned, copy = row_copy(i)

        @pl.when(owned)
        def _():
            copy.wait()

        return count

    lax.fori_loop(0, npts, issue, 0)
    lax.fori_loop(0, npts, drain, 0)
    block = picked[...]
    index = lax.broadcasted_iota(jnp.int32, block.shape, 0)
    chosen = jnp.where(index <= PRIOR, block, 0.0)
    both = dot(chosen[:, :split], chosen, ((0,), (0,)))
    rp = 2 * split // n
    for i in range(n):
        row, col = (i * rp) % split, (i * rp) // split * split
        out_ref[i, 0:rp, :] = both[row : row + rp, col : col + split]
    fresh = npts - PRIOR - 1
    out_ref[:, rp : rp + 1, :] = jnp.zeros((n, 1, split), jnp.float32)
    for i in range(fresh):
        for half in range(2):
            at = PRIOR + 1 + i
            out_ref[2 * i + half, rp : rp + 1, :] = picked[at : at + 1, half * split : (half + 1) * split]


def barrier_all(axes, n, me):
    barrier = pltpu.get_barrier_semaphore()

    def greet(off, carry):
        peer = lax.rem(me + off, n)
        pl.semaphore_signal(barrier, inc=1, device_id=coords(axes, peer), device_id_type=MESH)
        return carry

    lax.fori_loop(1, n, greet, 0)
    pl.semaphore_wait(barrier, n - 1)


def sweep_inverse(gram):
    size = gram.shape[0]
    tiles = [gram[8 * t : 8 * t + 8, :] for t in range(size // 8)]
    lane = lax.broadcasted_iota(jnp.int32, (8, size), 1)
    sub = lax.broadcasted_iota(jnp.int32, (8, size), 0)
    for k in range(size):
        t, s = k // 8, k % 8
        at_lane = lane == k
        row = jnp.broadcast_to(tiles[t][s : s + 1, :], (8, size))
        pivot = jnp.broadcast_to(row[:, k : k + 1], (8, size))
        inv = 1.0 / pivot
        scaled = jnp.where(at_lane, -inv, row * inv)
        fresh = []
        for r in range(size // 8):
            col = jnp.broadcast_to(tiles[r][:, k : k + 1], (8, size))
            fresh.append(jnp.where(at_lane, 0.0, tiles[r]) - col * scaled)
        fresh[t] = jnp.where(sub == s, scaled, fresh[t])
        tiles = fresh
    return -jnp.concatenate(tiles, axis=0)


def solve_kernel(axes, n, part_ref, hi_ref, lo_ref, landed, mine, full, square, send1, recv1, send2, recv2):
    me = flat_index(axes)
    rp = part_ref.shape[1] - 1
    split = part_ref.shape[2]
    barrier_all(axes, n, me)

    def scatter(off):
        peer = lax.rem(me + off, n)
        return pltpu.make_async_remote_copy(
            src_ref=part_ref.at[peer],
            dst_ref=landed.at[off],
            send_sem=send1.at[off],
            recv_sem=recv1.at[off],
            device_id=coords(axes, peer),
            device_id_type=MESH,
        )

    def spread(off):
        peer = lax.rem(me + off, n)
        return pltpu.make_async_remote_copy(
            src_ref=mine,
            dst_ref=full.at[me],
            send_sem=send2.at[off],
            recv_sem=recv2.at[off],
            device_id=coords(axes, peer),
            device_id_type=MESH,
        )

    def gathered(off):
        owner = lax.rem(me - off + n, n)
        return pltpu.make_async_remote_copy(
            src_ref=mine,
            dst_ref=full.at[owner],
            send_sem=send2.at[off],
            recv_sem=recv2.at[off],
            device_id=coords(axes, owner),
            device_id_type=MESH,
        )

    def loop(body):
        def step(off, carry):
            body(off)
            return carry

        lax.fori_loop(1, n, step, 0)

    loop(lambda off: scatter(off).start())
    loop(lambda off: scatter(off).wait_recv())
    total = part_ref[me]
    for off in range(1, n):
        total = total + landed[off]
    mine[...] = total
    full[me] = total
    loop(lambda off: scatter(off).wait_send())
    loop(lambda off: spread(off).start())
    loop(lambda off: gathered(off).wait_recv())
    loop(lambda off: spread(off).wait_send())

    for i in range(n):
        square[i * rp : (i + 1) * rp, :] = full[i, 0:rp, :]
    gram = square[0:split, :]
    cross = square[split : 2 * split, :]
    inverse = sweep_inverse(gram)
    coef = dot(inverse, cross)
    coef = coef + dot(inverse, cross - dot(gram, coef))
    left = [full[2 * i, rp : rp + 1, :] for i in range(3)]
    right = [full[2 * i + 1, rp : rp + 1, :] for i in range(3)]
    pad = jnp.zeros((5, split), jnp.float32)
    lefts = jnp.concatenate(left + [pad], axis=0)
    gains = dot(lefts, inverse)
    errors = dot(lefts, coef)
    kept = [coef]
    ks, ss, ds = [], [], []
    for j in range(3):
        k = gains[j : j + 1, :]
        d = right[j] - errors[j : j + 1, :]
        for k0, s0, d0 in zip(ks, ss, ds):
            along = jnp.sum(k0 * left[j], axis=1, keepdims=True)
            k = k - k0 * (along / s0)
            d = d - along * d0
        s = 1.0 + jnp.sum(k * left[j], axis=1, keepdims=True)
        d = d / s
        ks.append(k)
        ss.append(s)
        ds.append(d)
        pad7 = jnp.zeros((7, split), jnp.float32)
        coef = coef + dot(
            jnp.concatenate([k, pad7], axis=0), jnp.concatenate([d, pad7], axis=0), ((0,), (0,))
        )
        kept.append(coef)
    for j, value in enumerate(kept):
        hi = value.astype(jnp.bfloat16)
        hi_ref[:, j * split : (j + 1) * split] = hi
        lo_ref[:, j * split : (j + 1) * split] = (value - hi.astype(jnp.float32)).astype(jnp.bfloat16)


def residual_kernel(modes_ref, hi_ref, lo_ref, res_ref, sums_ref):
    split = res_ref.shape[1]
    steps = hi_ref.shape[1] // split
    fit = modes_ref[:, :split]
    rest = modes_ref[:, split:]
    hi = fit.astype(jnp.bfloat16)
    lo = (fit - hi.astype(jnp.float32)).astype(jnp.bfloat16)
    wide = jnp.concatenate([hi, lo], axis=1)
    top = hi_ref[...]
    f32 = jnp.float32
    made = jnp.dot(wide, jnp.concatenate([top, top], axis=0), preferred_element_type=f32)
    made = made + jnp.dot(hi, lo_ref[...], preferred_element_type=f32)

    @pl.when(pl.program_id(0) == 0)
    def _():
        sums_ref[...] = jnp.zeros_like(sums_ref)

    for j in range(steps):
        left = rest - made[:, j * split : (j + 1) * split]
        if j == steps - 1:
            res_ref[...] = left
        part = jnp.sum((left * left).reshape(-1, 8, split), axis=0)
        sums_ref[8 * j : 8 * j + 8, :] += part


def norm_kernel(axes, n, total_rows, sums_ref, out_ref, landed, mine, send, recv):
    me = flat_index(axes)
    steps = out_ref.shape[0]
    for j in range(steps):
        mine[j : j + 1, :] = jnp.sum(sums_ref[8 * j : 8 * j + 8, :], axis=0, keepdims=True)
    barrier_all(axes, n, me)

    def share(off):
        peer = lax.rem(me + off, n)
        return pltpu.make_async_remote_copy(
            src_ref=mine,
            dst_ref=landed.at[me],
            send_sem=send.at[off],
            recv_sem=recv.at[off],
            device_id=coords(axes, peer),
            device_id_type=MESH,
        )

    def arrival(off):
        owner = lax.rem(me - off + n, n)
        return pltpu.make_async_remote_copy(
            src_ref=mine,
            dst_ref=landed.at[owner],
            send_sem=send.at[off],
            recv_sem=recv.at[off],
            device_id=coords(axes, owner),
            device_id_type=MESH,
        )

    def loop(body):
        def step(off, carry):
            body(off)
            return carry

        lax.fori_loop(1, n, step, 0)

    loop(lambda off: share(off).start())
    landed[me] = mine[...]
    loop(lambda off: arrival(off).wait_recv())
    total = landed[0]
    for i in range(1, n):
        total = total + landed[i]
    out_ref[...] = total / total_rows
    loop(lambda off: share(off).wait_send())


def on_device(axes, modes, points):
    n = axes[0][1] * axes[1][1]
    rows_dev, cols = modes.shape
    split = cols // 2
    rp = 2 * split // n
    npts = points.shape[0]
    steps = npts - PRIOR
    padded = -(-npts // 8) * 8
    f32 = jnp.float32
    vmem = pl.BlockSpec(memory_space=pltpu.VMEM)
    part = pl.pallas_call(
        functools.partial(pick_kernel, axes, n),
        out_shape=jax.ShapeDtypeStruct((n, rp + 1, split), f32),
        in_specs=[pl.BlockSpec(memory_space=pltpu.SMEM), pl.BlockSpec(memory_space=pl.ANY)],
        out_specs=vmem,
        scratch_shapes=[pltpu.VMEM((padded, cols), f32), pltpu.SemaphoreType.DMA],
        name="pick",
    )(points, modes)
    hi, lo = pl.pallas_call(
        functools.partial(solve_kernel, axes, n),
        out_shape=[jax.ShapeDtypeStruct((split, steps * split), jnp.bfloat16)] * 2,
        in_specs=[vmem],
        out_specs=[vmem, vmem],
        scratch_shapes=[
            pltpu.VMEM((n, rp + 1, split), f32),
            pltpu.VMEM((rp + 1, split), f32),
            pltpu.VMEM((n, rp + 1, split), f32),
            pltpu.VMEM((2 * split, split), f32),
        ]
        + [pltpu.SemaphoreType.DMA((n,))] * 4,
        compiler_params=pltpu.CompilerParams(collective_id=0, has_side_effects=True),
        name="solve",
    )(part)
    tile = 2048 if rows_dev % 2048 == 0 else rows_dev
    residual, sums = pl.pallas_call(
        residual_kernel,
        grid=(rows_dev // tile,),
        out_shape=[jax.ShapeDtypeStruct((rows_dev, split), f32), jax.ShapeDtypeStruct((8 * steps, split), f32)],
        in_specs=[
            pl.BlockSpec((tile, cols), lambda i: (i, 0)),
            pl.BlockSpec((split, steps * split), lambda i: (0, 0)),
            pl.BlockSpec((split, steps * split), lambda i: (0, 0)),
        ],
        out_specs=[pl.BlockSpec((tile, split), lambda i: (i, 0)), pl.BlockSpec((8 * steps, split), lambda i: (0, 0))],
        name="residual",
    )(modes, hi, lo)
    norms = pl.pallas_call(
        functools.partial(norm_kernel, axes, n, rows_dev * n),
        out_shape=jax.ShapeDtypeStruct((steps, split), f32),
        in_specs=[vmem],
        out_specs=vmem,
        scratch_shapes=[
            pltpu.VMEM((n, steps, split), f32),
            pltpu.VMEM((steps, split), f32),
            pltpu.SemaphoreType.DMA((n,)),
            pltpu.SemaphoreType.DMA((n,)),
        ],
        compiler_params=pltpu.CompilerParams(collective_id=1, has_side_effects=True),
        name="norms",
    )(sums)
    return residual, norms


def solution(mesh):
    axes = tuple((name, mesh.shape[name]) for name in ("rows", "grp"))
    return jax.shard_map(
        functools.partial(on_device, axes),
        mesh=mesh,
        in_specs=(P(("rows", "grp"), None), P()),
        out_specs=(P(("rows", "grp"), None), P()),
        check_vma=False,
    )
```

time: 299 us -> 72.5 us (0.24); the launches traced: 294 us -> 72.2 us
  other arithmetic: 97.9 us -> 0 us
  waiting for transfers between devices: 74 us -> 0 us
  Pallas kernels: 0 us -> 70.3 us
  blocking collectives: 42.2 us -> 0 us
  matrix products: 40.9 us -> 0 us
  local copies, waits for them, and re-layouts: 24.6 us -> 1.23 us
  between operations: 14.5 us -> 0.65 us
    another operation x22 -> x0, other arithmetic: 92.4 us -> none  [the longest x12 49.6 us: on_device(): factor = jnp.linalg.cholesky(gram)]
    psum x1 -> x0, waiting for transfers between devices: 74 us -> none  [on_device(): lax.psum((picked, local_ftf, local_ftr, local_sq), ('rows', 'grp'))]
    pallas_call x0 -> x4, Pallas kernels: none -> 70.3 us  [the longest x1 39.6 us: on_device(): pl.pallas_call(functools.partial(solve_kernel, axes, n), out_shape=[jax.S...]
    psum x1 -> x0, blocking collectives: 42.2 us -> none  [on_device(): lax.psum((picked, local_ftf, local_ftr, local_sq), ('rows', 'grp'))]
    dot_general x9 -> x0, matrix products: 38.7 us -> none  [the longest x1 14 us: on_device(): jnp.dot(fit_modes.T, rest_modes, preferred_element_type=jnp.float32, prec...]
    unnamed x9 -> x1, local copies, waits for them, and re-layouts: 18 us -> 1.23 us
    gather x1 -> x0, local copies, waits for them, and re-layouts: 5.44 us -> none  [on_device(): picked = jnp.where(owned[:, None], modes[safe_idx], 0.0)]
    reduce_sum x1 -> x0, other arithmetic: 3.3 us -> none  [on_device(): local_sq = jnp.sum(rest_modes * rest_modes, axis=0)]
  transfers between devices with their start and end apart: 1 -> 0, of which waited for: 1 -> 0; matrix products, arithmetic and copies ran while one was open for 5% -> 0% of each run, Pallas kernels for 0% -> 0%
where the time goes in v1:
time: 72.5 us; the launch traced here: 72.2 us
  Pallas kernels  70.3 us (97%)
  local copies, waits for them, and re-layouts  1.23 us (2%)
    pallas_call x1, Pallas kernels, on_device(): pl.pallas_call(functools.partial(solve_kernel, axes, n), out_shape=[jax.S...  39.6 us
    pallas_call x1, Pallas kernels, on_device(): pl.pallas_call(residual_kernel, grid=(rows_dev // tile,), out_shape=[jax....  15 us
    pallas_call x1, Pallas kernels, on_device(): pl.pallas_call(functools.partial(norm_kernel, axes, n, rows_dev * n), out...  9.88 us
    pallas_call x1, Pallas kernels, on_device(): pl.pallas_call(functools.partial(pick_kernel, axes, n), out_shape=jax.Sha...  5.85 us

profile of v1, /device:TPU:0, one launch (start us, length us, event | category | flops | bytes accessed | tf_op | source)
XLA Modules:
  0.0 72.2 jit_solution(1555783855236012220)
XLA Ops:
  0.6 5.9 %pick.1.part_ref = f32[32,9,128]{2,1,0:T(8,128)} custom-call(s32[196]{0:T(256)} %points_ref.1, f32[12288,256]{1,0:T(8,128)} %modes_ref.3), custom_call_target="tpu_custom_call" | custom-call | tf_op jit(solution)/shard_map/pick/pallas_call | solution.py:291
  6.5 39.6 %solve.1 = (bf16[128,512]{1,0:T(8,128)(2,1)}, bf16[128,512]{1,0:T(8,128)(2,1)}) custom-call(f32[32,9,128]{2,1,0:T(8,128)} %pick.1.part_ref), custom_call_target="tpu_custom_call" | custom-call | tf_op jit(solution)/shard_map/solve/pallas_call | solution.py:299
  46.1 15.0 %residual.1 = (f32[12288,128]{1,0:T(8,128)}, f32[32,128]{1,0:T(8,128)}) custom-call(f32[12288,256]{1,0:T(8,128)} %modes_ref.3, bf16[128,512]{1,0:T(8,128)(2,1)} %get-tuple-element.6.hi_ref, bf16[128,512]{1,0:T(8,128)(2,1)} %get-tuple-element.7.lo_ref), custom_call_target="tpu_custom_call" | custom-call | tf_op jit(solution)/shard_map/residual/pallas_call | solution.py:315
  61.1 9.9 %norms.1 = f32[4,128]{1,0:T(4,128)} custom-call(f32[32,128]{1,0:T(8,128)} %get-tuple-element.9.sums_ref), custom_call_target="tpu_custom_call" | custom-call | tf_op jit(solution)/shard_map/norms/pallas_call | solution.py:327
  71.0 1.2 %copy.5 = f32[4,128]{1,0:T(4,128)} copy(f32[4,128]{1,0:T(4,128)} %norms.1) | data formatting | bytes 4096

commit v2 on v1

--- a/solution.py
+++ b/solution.py
@@ -8,7 +8,7 @@
 from jax.sharding import PartitionSpec as P
 
 PRIOR = 192
-LANES = 128
+BLOCK = 8
 HIGH = lax.Precision.HIGHEST
 MESH = pl.DeviceIdType.MESH
 
@@ -90,28 +90,65 @@
     pl.semaphore_wait(barrier, n - 1)
 
 
-def sweep_inverse(gram):
+def small_inverse(e):
+    size = len(e)
+    e = [list(line) for line in e]
+    for p in range(size):
+        inv = 1.0 / e[p][p]
+        line = [e[p][j] * inv for j in range(size)]
+        line[p] = -inv
+        for i in range(size):
+            for j in range(i, size):
+                if i == p or j == p:
+                    continue
+                e[i][j] = e[i][j] - e[p][i] * line[j]
+                e[j][i] = e[i][j]
+        for j in range(size):
+            e[p][j] = line[j]
+            e[j][p] = line[j]
+    return [[-value for value in line] for line in e]
+
+
+def sweep_inverse(gram, width=BLOCK):
     size = gram.shape[0]
+    shape = (8, size)
     tiles = [gram[8 * t : 8 * t + 8, :] for t in range(size // 8)]
-    lane = lax.broadcasted_iota(jnp.int32, (8, size), 1)
-    sub = lax.broadcasted_iota(jnp.int32, (8, size), 0)
-    for k in range(size):
+    lane = lax.broadcasted_iota(jnp.int32, shape, 1)
+    sub = lax.broadcasted_iota(jnp.int32, shape, 0)
+    for k in range(0, size, width):
         t, s = k // 8, k % 8
-        at_lane = lane == k
-        row = jnp.broadcast_to(tiles[t][s : s + 1, :], (8, size))
-        pivot = jnp.broadcast_to(row[:, k : k + 1], (8, size))
-        inv = 1.0 / pivot
-        scaled = jnp.where(at_lane, -inv, row * inv)
+        inside = (lane >= k) & (lane < k + width)
+        own = [jnp.broadcast_to(tiles[t][:, k + q : k + q + 1], shape) for q in range(width)]
+        entry = [[None] * width for _ in range(width)]
+        for p in range(width):
+            for q in range(p, width):
+                entry[p][q] = jnp.broadcast_to(own[q][s + p : s + p + 1, :], shape)
+                entry[q][p] = entry[p][q]
+        small = small_inverse(entry)
+        rows = []
+        for q in range(width):
+            row = jnp.broadcast_to(tiles[t][s + q : s + q + 1, :], shape)
+            rows.append(jnp.where(inside, jnp.where(lane == k + q, -1.0, 0.0), row))
+        scaled = []
+        for p in range(width):
+            line = small[p][0] * rows[0]
+            for q in range(1, width):
+                line = line + small[p][q] * rows[q]
+            scaled.append(line)
         fresh = []
         for r in range(size // 8):
-            col = jnp.broadcast_to(tiles[r][:, k : k + 1], (8, size))
-            fresh.append(jnp.where(at_lane, 0.0, tiles[r]) - col * scaled)
-        fresh[t] = jnp.where(sub == s, scaled, fresh[t])
+            value = jnp.where(inside, 0.0, tiles[r])
+            for p in range(width):
+                col = own[p] if r == t else jnp.broadcast_to(tiles[r][:, k + p : k + p + 1], shape)
+                value = value - col * scaled[p]
+            fresh.append(value)
+        for p in range(width):
+            fresh[t] = jnp.where(sub == s + p, scaled[p], fresh[t])
         tiles = fresh
     return -jnp.concatenate(tiles, axis=0)
 
 
-def solve_kernel(axes, n, part_ref, hi_ref, lo_ref, landed, mine, full, square, send1, recv1, send2, recv2):
+def solve_kernel(axes, n, part_ref, wide_ref, delta_ref, landed, mine, full, square, send1, recv1, send2, recv2):
     me = flat_index(axes)
     rp = part_ref.shape[1] - 1
     split = part_ref.shape[2]
@@ -182,7 +219,6 @@
     lefts = jnp.concatenate(left + [pad], axis=0)
     gains = dot(lefts, inverse)
     errors = dot(lefts, coef)
-    kept = [coef]
     ks, ss, ds = [], [], []
     for j in range(3):
         k = gains[j : j + 1, :]
@@ -196,40 +232,55 @@
         ks.append(k)
         ss.append(s)
         ds.append(d)
-        pad7 = jnp.zeros((7, split), jnp.float32)
-        coef = coef + dot(
-            jnp.concatenate([k, pad7], axis=0), jnp.concatenate([d, pad7], axis=0), ((0,), (0,))
-        )
-        kept.append(coef)
-    for j, value in enumerate(kept):
-        hi = value.astype(jnp.bfloat16)
-        hi_ref[:, j * split : (j + 1) * split] = hi
-        lo_ref[:, j * split : (j + 1) * split] = (value - hi.astype(jnp.float32)).astype(jnp.bfloat16)
-
-
-def residual_kernel(modes_ref, hi_ref, lo_ref, res_ref, sums_ref):
+    gain = jnp.concatenate(ks + [pad], axis=0)
+    delta = jnp.concatenate(ds + [pad], axis=0)
+    coef = coef + dot(gain, delta, ((0,), (0,)))
+    delta_ref[...] = delta
+    full_gain = jnp.transpose(jnp.concatenate([gain, jnp.zeros((split - 8, split), jnp.float32)], axis=0))
+    zero = jnp.zeros((split, split), jnp.bfloat16)
+    c_hi, c_lo = halves(coef)
+    k_hi, k_lo = halves(full_gain)
+    wide_ref[0:split, 0:split] = c_hi
+    wide_ref[split:, 0:split] = c_hi
+    wide_ref[0:split, split : 2 * split] = c_lo
+    wide_ref[split:, split : 2 * split] = zero
+    wide_ref[0:split, 2 * split : 3 * split] = k_hi
+    wide_ref[split:, 2 * split : 3 * split] = k_hi
+    wide_ref[0:split, 3 * split :] = k_lo
+    wide_ref[split:, 3 * split :] = zero
+
+
+def halves(value):
+    hi = value.astype(jnp.bfloat16)
+    return hi, (value - hi.astype(jnp.float32)).astype(jnp.bfloat16)
+
+
+def residual_kernel(modes_ref, wide_ref, delta_ref, res_ref, sums_ref):
     split = res_ref.shape[1]
-    steps = hi_ref.shape[1] // split
-    fit = modes_ref[:, :split]
-    rest = modes_ref[:, split:]
-    hi = fit.astype(jnp.bfloat16)
-    lo = (fit - hi.astype(jnp.float32)).astype(jnp.bfloat16)
-    wide = jnp.concatenate([hi, lo], axis=1)
-    top = hi_ref[...]
-    f32 = jnp.float32
-    made = jnp.dot(wide, jnp.concatenate([top, top], axis=0), preferred_element_type=f32)
-    made = made + jnp.dot(hi, lo_ref[...], preferred_element_type=f32)
+    steps = sums_ref.shape[0] // 8
 
     @pl.when(pl.program_id(0) == 0)
     def _():
         sums_ref[...] = jnp.zeros_like(sums_ref)
 
+    rows = res_ref.shape[0]
+    chunk = 256 if rows % 256 == 0 else rows
+    wide = wide_ref[...]
+    deltas = [delta_ref[j : j + 1, :] for j in range(steps - 1)]
+    totals = [sums_ref[8 * j : 8 * j + 8, :] for j in range(steps)]
+    for at in range(0, rows, chunk):
+        hi, lo = halves(modes_ref[at : at + chunk, :split])
+        pair = jnp.concatenate([hi, lo], axis=1)
+        made = jnp.dot(pair, wide, preferred_element_type=jnp.float32)
+        left = modes_ref[at : at + chunk, split:] - (made[:, :split] + made[:, split : 2 * split])
+        res_ref[at : at + chunk, :] = left
+        along = made[:, 2 * split : 3 * split] + made[:, 3 * split :]
+        for j in range(steps - 1, -1, -1):
+            totals[j] = totals[j] + jnp.sum((left * left).reshape(-1, 8, split), axis=0)
+            if j:
+                left = left + along[:, j - 1 : j] * deltas[j - 1]
     for j in range(steps):
-        left = rest - made[:, j * split : (j + 1) * split]
-        if j == steps - 1:
-            res_ref[...] = left
-        part = jnp.sum((left * left).reshape(-1, 8, split), axis=0)
-        sums_ref[8 * j : 8 * j + 8, :] += part
+        sums_ref[8 * j : 8 * j + 8, :] = totals[j]
 
 
 def norm_kernel(axes, n, total_rows, sums_ref, out_ref, landed, mine, send, recv):
@@ -296,9 +347,9 @@
         scratch_shapes=[pltpu.VMEM((padded, cols), f32), pltpu.SemaphoreType.DMA],
         name="pick",
     )(points, modes)
-    hi, lo = pl.pallas_call(
+    wide, delta = pl.pallas_call(
         functools.partial(solve_kernel, axes, n),
-        out_shape=[jax.ShapeDtypeStruct((split, steps * split), jnp.bfloat16)] * 2,
+        out_shape=[jax.ShapeDtypeStruct((2 * split, 4 * split), jnp.bfloat16), jax.ShapeDtypeStruct((8, split), f32)],
         in_specs=[vmem],
         out_specs=[vmem, vmem],
         scratch_shapes=[
@@ -318,12 +369,12 @@
         out_shape=[jax.ShapeDtypeStruct((rows_dev, split), f32), jax.ShapeDtypeStruct((8 * steps, split), f32)],
         in_specs=[
             pl.BlockSpec((tile, cols), lambda i: (i, 0)),
-            pl.BlockSpec((split, steps * split), lambda i: (0, 0)),
-            pl.BlockSpec((split, steps * split), lambda i: (0, 0)),
+            pl.BlockSpec((2 * split, 4 * split), lambda i: (0, 0)),
+            pl.BlockSpec((8, split), lambda i: (0, 0)),
         ],
         out_specs=[pl.BlockSpec((tile, split), lambda i: (i, 0)), pl.BlockSpec((8 * steps, split), lambda i: (0, 0))],
         name="residual",
-    )(modes, hi, lo)
+    )(modes, wide, delta)
     norms = pl.pallas_call(
         functools.partial(norm_kernel, axes, n, rows_dev * n),
         out_shape=jax.ShapeDtypeStruct((steps, split), f32),

time: 72.5 us -> 55.9 us (0.77)
  Pallas kernels: 70.3 us -> 53.7 us
    pallas_call x1, Pallas kernels: 39.6 us -> 27.3 us  [on_device(): pl.pallas_call(functools.partial(solve_kernel, axes, n), out_shape=[jax.S...]
    pallas_call x1, Pallas kernels: 15 us -> 10.6 us  [on_device(): pl.pallas_call(residual_kernel, grid=(rows_dev // tile,), out_shape=[jax....]
where the time goes in v2:
time: 55.9 us; the launch traced here: 55.5 us
  Pallas kernels  53.7 us (96%)
  local copies, waits for them, and re-layouts  1.23 us (2%)
  between operations  0.65 us (1%)
    pallas_call x1, Pallas kernels, on_device(): pl.pallas_call(functools.partial(solve_kernel, axes, n), out_shape=[jax.S...  27.3 us
    pallas_call x1, Pallas kernels, on_device(): pl.pallas_call(residual_kernel, grid=(rows_dev // tile,), out_shape=[jax....  10.6 us
    pallas_call x1, Pallas kernels, on_device(): pl.pallas_call(functools.partial(norm_kernel, axes, n, rows_dev * n), out...  9.88 us
    pallas_call x1, Pallas kernels, on_device(): pl.pallas_call(functools.partial(pick_kernel, axes, n), out_shape=jax.Sha...  5.85 us
    unnamed x1, local copies, waits for them, and re-layouts  1.23 us

profile of v2, /device:TPU:0, one launch (start us, length us, event | category | flops | bytes accessed | tf_op | source)
XLA Modules:
  0.0 55.5 jit_solution(1354872026201468543)
XLA Ops:
  0.6 5.9 %pick.1.part_ref = f32[32,9,128]{2,1,0:T(8,128)} custom-call(s32[196]{0:T(256)} %points_ref.1, f32[12288,256]{1,0:T(8,128)} %modes_ref.3), custom_call_target="tpu_custom_call" | custom-call | tf_op jit(solution)/shard_map/pick/pallas_call | solution.py:342
  6.5 27.3 %solve.1 = (bf16[256,512]{1,0:T(8,128)(2,1)}, f32[8,128]{1,0:T(8,128)}) custom-call(f32[32,9,128]{2,1,0:T(8,128)} %pick.1.part_ref), custom_call_target="tpu_custom_call" | custom-call | tf_op jit(solution)/shard_map/solve/pallas_call | solution.py:350
  33.8 10.6 %residual.1 = (f32[12288,128]{1,0:T(8,128)}, f32[32,128]{1,0:T(8,128)}) custom-call(f32[12288,256]{1,0:T(8,128)} %modes_ref.3, bf16[256,512]{1,0:T(8,128)(2,1)} %get-tuple-element.6.wide_ref, f32[8,128]{1,0:T(8,128)} %get-tuple-element.7.delta_ref), custom_call_target="tpu_custom_call" | custom-call | tf_op jit(solution)/shard_map/residual/pallas_call | solution.py:366
  44.4 9.9 %norms.1 = f32[4,128]{1,0:T(4,128)} custom-call(f32[32,128]{1,0:T(8,128)} %get-tuple-element.9.sums_ref), custom_call_target="tpu_custom_call" | custom-call | tf_op jit(solution)/shard_map/norms/pallas_call | solution.py:378
  54.3 1.2 %copy.5 = f32[4,128]{1,0:T(4,128)} copy(f32[4,128]{1,0:T(4,128)} %norms.1) | data formatting | bytes 4096

commit v3 on v2

v3 whole, which is shorter than its diff:
```python
import functools

import jax
import jax.numpy as jnp
from jax import lax
from jax.experimental import pallas as pl
from jax.experimental.pallas import tpu as pltpu
from jax.sharding import PartitionSpec as P

PRIOR = 192
BLOCK = 8
HOOK_AT = 80
FIRST, SECOND = 4, 8
HIGH = lax.Precision.HIGHEST
MESH = pl.DeviceIdType.MESH


def dot(a, b, dims=((1,), (0,))):
    return lax.dot_general(a, b, (dims, ((), ())), precision=HIGH, preferred_element_type=jnp.float32)


def flat_index(axes):
    (first, _), (second, width) = axes
    return lax.axis_index(first) * width + lax.axis_index(second)


def coords(axes, flat):
    width = axes[1][1]
    return (flat // width, lax.rem(flat, width))


def pick_kernel(axes, n, points_ref, modes_ref, out_ref, picked, sem):
    rows_dev, cols = modes_ref.shape
    npts = points_ref.shape[0]
    split = cols // 2
    base = flat_index(axes) * rows_dev
    picked[...] = jnp.zeros_like(picked)

    def row_copy(i):
        local = points_ref[i] - base
        owned = (local >= 0) & (local < rows_dev)
        safe = jnp.clip(local, 0, rows_dev - 1)
        return owned, pltpu.make_async_copy(
            modes_ref.at[pl.ds(safe, 1), :], picked.at[pl.ds(i, 1), :], sem
        )

    def issue(i, count):
        owned, copy = row_copy(i)

        @pl.when(owned)
        def _():
            copy.start()

        return count

    def drain(i, count):
        owned, copy = row_copy(i)

        @pl.when(owned)
        def _():
            copy.wait()

        return count

    lax.fori_loop(0, npts, issue, 0)
    lax.fori_loop(0, npts, drain, 0)
    block = picked[...]
    index = lax.broadcasted_iota(jnp.int32, block.shape, 0)
    chosen = jnp.where(index <= PRIOR, block, 0.0)
    both = dot(chosen[:, :split], chosen, ((0,), (0,)))
    rp = 2 * split // n
    for i in range(n):
        row, col = (i * rp) % split, (i * rp) // split * split
        out_ref[i, 0:rp, :] = both[row : row + rp, col : col + split]
    fresh = npts - PRIOR - 1
    out_ref[:, rp : rp + 1, :] = jnp.zeros((n, 1, split), jnp.float32)
    for i in range(fresh):
        for half in range(2):
            at = PRIOR + 1 + i
            out_ref[2 * i + half, rp : rp + 1, :] = picked[at : at + 1, half * split : (half + 1) * split]


def barrier_all(axes, n, me):
    barrier = pltpu.get_barrier_semaphore()

    def greet(off, carry):
        peer = lax.rem(me + off, n)
        pl.semaphore_signal(barrier, inc=1, device_id=coords(axes, peer), device_id_type=MESH)
        return carry

    lax.fori_loop(1, n, greet, 0)
    pl.semaphore_wait(barrier, n - 1)


def small_inverse(e):
    size = len(e)
    e = [list(line) for line in e]
    for p in range(size):
        inv = 1.0 / e[p][p]
        line = [e[p][j] * inv for j in range(size)]
        line[p] = -inv
        for i in range(size):
            for j in range(i, size):
                if i == p or j == p:
                    continue
                e[i][j] = e[i][j] - e[p][i] * line[j]
                e[j][i] = e[i][j]
        for j in range(size):
            e[p][j] = line[j]
            e[j][p] = line[j]
    return [[-value for value in line] for line in e]


def sweep_inverse(gram, hook, width=BLOCK):
    size = gram.shape[0]
    shape = (8, size)
    tiles = [gram[8 * t : 8 * t + 8, :] for t in range(size // 8)]
    lane = lax.broadcasted_iota(jnp.int32, shape, 1)
    sub = lax.broadcasted_iota(jnp.int32, shape, 0)
    for k in range(0, size, width):
        if k == HOOK_AT:
            hook()
        t, s = k // 8, k % 8
        inside = (lane >= k) & (lane < k + width)
        own = [jnp.broadcast_to(tiles[t][:, k + q : k + q + 1], shape) for q in range(width)]
        entry = [[None] * width for _ in range(width)]
        for p in range(width):
            for q in range(p, width):
                entry[p][q] = jnp.broadcast_to(own[q][s + p : s + p + 1, :], shape)
                entry[q][p] = entry[p][q]
        small = small_inverse(entry)
        rows = []
        for q in range(width):
            row = jnp.broadcast_to(tiles[t][s + q : s + q + 1, :], shape)
            rows.append(jnp.where(inside, jnp.where(lane == k + q, -1.0, 0.0), row))
        scaled = []
        for p in range(width):
            line = small[p][0] * rows[0]
            for q in range(1, width):
                line = line + small[p][q] * rows[q]
            scaled.append(line)
        fresh = []
        for r in range(size // 8):
            value = jnp.where(inside, 0.0, tiles[r])
            for p in range(width):
                col = own[p] if r == t else jnp.broadcast_to(tiles[r][:, k + p : k + p + 1], shape)
                value = value - col * scaled[p]
            fresh.append(value)
        for p in range(width):
            fresh[t] = jnp.where(sub == s + p, scaled[p], fresh[t])
        tiles = fresh
    return -jnp.concatenate(tiles, axis=0)


def solve_kernel(
    axes, n, part_ref, modes_ref, wide_ref, norm_ref,
    landed, mine, full, part2, landed2, mine2, full2, square, held, acc, squares,
    send1, recv1, send2, recv2, local,
):
    me = flat_index(axes)
    rp = part_ref.shape[1] - 1
    split = part_ref.shape[2]
    steps = norm_ref.shape[0]
    chunks, rows = held.shape[0], held.shape[1]
    total_rows = chunks * rows * n

    def loop(body, first=1, last=n):
        def step(off, carry):
            body(off)
            return carry

        lax.fori_loop(first, last, step, 0)

    def fetch(c):
        return pltpu.make_async_copy(
            modes_ref.at[pl.ds(c * rows, rows), :], held.at[c], local.at[c]
        )

    loop(lambda c: fetch(c).start(), 0, chunks)
    barrier = pltpu.get_barrier_semaphore()

    def greet(off):
        peer = lax.rem(me + off, n)
        pl.semaphore_signal(barrier, inc=1, device_id=coords(axes, peer), device_id_type=MESH)

    loop(greet)
    acc[...] = jnp.zeros_like(acc)
    squares[...] = jnp.zeros_like(squares)

    def grams(c):
        fetch(c).wait()
        acc[...] += dot(held[c, :, :split], held[c], ((0,), (0,)))
        rest = held[c, :, split:]
        squares[...] += jnp.sum((rest * rest).reshape(-1, 8, split), axis=0)

    def scatter(src, dst, off):
        peer = lax.rem(me + off, n)
        return pltpu.make_async_remote_copy(
            src_ref=src.at[peer],
            dst_ref=dst.at[off],
            send_sem=send1.at[off],
            recv_sem=recv1.at[off],
            device_id=coords(axes, peer),
            device_id_type=MESH,
        )

    def spread(src, dst, off):
        peer = lax.rem(me + off, n)
        return pltpu.make_async_remote_copy(
            src_ref=src,
            dst_ref=dst.at[me],
            send_sem=send2.at[off],
            recv_sem=recv2.at[off],
            device_id=coords(axes, peer),
            device_id_type=MESH,
        )

    def gathered(src, dst, off):
        owner = lax.rem(me - off + n, n)
        return pltpu.make_async_remote_copy(
            src_ref=src,
            dst_ref=dst.at[owner],
            send_sem=send2.at[off],
            recv_sem=recv2.at[off],
            device_id=coords(axes, owner),
            device_id_type=MESH,
        )

    def reduced(src, got, own, whole):
        loop(lambda off: scatter(src, got, off).wait_recv())
        total = src[me]
        for off in range(1, n):
            total = total + got[off]
        own[...] = total
        whole[me] = total
        loop(lambda off: scatter(src, got, off).wait_send())
        loop(lambda off: spread(own, whole, off).start())

    def finish(own, whole):
        loop(lambda off: gathered(own, whole, off).wait_recv())
        loop(lambda off: spread(own, whole, off).wait_send())
        for i in range(n):
            square[i * rp : (i + 1) * rp, :] = whole[i, 0:rp, :]
        return square[0:split, :], square[split : 2 * split, :]

    first, second = min(FIRST, chunks), min(SECOND, chunks)
    pl.semaphore_wait(barrier, n - 1)
    loop(lambda off: scatter(part_ref, landed, off).start())
    loop(grams, 0, first)
    reduced(part_ref, landed, mine, full)
    loop(grams, first, chunks)
    part2[...] = jnp.zeros_like(part2)
    for i in range(n):
        row, col = (i * rp) % split, (i * rp) // split * split
        part2[i, 0:rp, :] = acc[row : row + rp, col : col + split]
    part2[0, rp : rp + 1, :] = jnp.sum(squares[...], axis=0, keepdims=True)
    gram, cross = finish(mine, full)
    loop(lambda off: scatter(part2, landed2, off).start())
    inverse = sweep_inverse(gram, lambda: reduced(part2, landed2, mine2, full2))
    coef = dot(inverse, cross)
    coef = coef + dot(inverse, cross - dot(gram, coef))
    left = [full[2 * i, rp : rp + 1, :] for i in range(3)]
    right = [full[2 * i + 1, rp : rp + 1, :] for i in range(3)]
    pad = jnp.zeros((5, split), jnp.float32)
    lefts = jnp.concatenate(left + [pad], axis=0)
    gains = dot(lefts, inverse)
    errors = dot(lefts, coef)
    ks, ss, ds = [], [], []
    kept = [coef]
    pad7 = jnp.zeros((7, split), jnp.float32)
    for j in range(3):
        k = gains[j : j + 1, :]
        d = right[j] - errors[j : j + 1, :]
        for k0, s0, d0 in zip(ks, ss, ds):
            along = jnp.sum(k0 * left[j], axis=1, keepdims=True)
            k = k - k0 * (along / s0)
            d = d - along * d0
        s = 1.0 + jnp.sum(k * left[j], axis=1, keepdims=True)
        d = d / s
        ks.append(k)
        ss.append(s)
        ds.append(d)
        turn = dot(jnp.concatenate([k, pad7], axis=0), jnp.concatenate([d, pad7], axis=0), ((0,), (0,)))
        kept.append(kept[-1] + turn)
    c_hi, c_lo = halves(kept[-1])
    wide_ref[0:split, 0:split] = c_hi
    wide_ref[split:, 0:split] = c_hi
    wide_ref[0:split, split : 2 * split] = c_lo
    wide_ref[split:, split : 2 * split] = jnp.zeros((split, split), jnp.bfloat16)
    ftf, ftr = finish(mine2, full2)
    sq = full2[0, rp : rp + 1, :]
    curved = dot(ftf, jnp.concatenate(kept, axis=1))
    for j in range(steps):
        bent = kept[j] * (curved[:, j * split : (j + 1) * split] - 2.0 * ftr)
        norm_ref[j : j + 1, :] = (sq + jnp.sum(bent, axis=0, keepdims=True)) / total_rows


def halves(value):
    hi = value.astype(jnp.bfloat16)
    return hi, (value - hi.astype(jnp.float32)).astype(jnp.bfloat16)


def residual_kernel(modes_ref, wide_ref, res_ref):
    rows, split = res_ref.shape
    chunk = 256 if rows % 256 == 0 else rows
    wide = wide_ref[...]
    for at in range(0, rows, chunk):
        hi, lo = halves(modes_ref[at : at + chunk, :split])
        pair = jnp.concatenate([hi, lo], axis=1)
        made = jnp.dot(pair, wide, preferred_element_type=jnp.float32)
        res_ref[at : at + chunk, :] = modes_ref[at : at + chunk, split:] - (made[:, :split] + made[:, split:])


def on_device(axes, modes, points):
    n = axes[0][1] * axes[1][1]
    rows_dev, cols = modes.shape
    split = cols // 2
    rp = 2 * split // n
    npts = points.shape[0]
    steps = npts - PRIOR
    padded = -(-npts // 8) * 8
    f32 = jnp.float32
    vmem = pl.BlockSpec(memory_space=pltpu.VMEM)
    part = pl.pallas_call(
        functools.partial(pick_kernel, axes, n),
        out_shape=jax.ShapeDtypeStruct((n, rp + 1, split), f32),
        in_specs=[pl.BlockSpec(memory_space=pltpu.SMEM), pl.BlockSpec(memory_space=pl.ANY)],
        out_specs=vmem,
        scratch_shapes=[pltpu.VMEM((padded, cols), f32), pltpu.SemaphoreType.DMA],
        name="pick",
    )(points, modes)
    chunks = 12 if rows_dev % 96 == 0 else 1
    chunk_shape = pltpu.VMEM((n, rp + 1, split), f32)
    own_shape = pltpu.VMEM((rp + 1, split), f32)
    wide, norms = pl.pallas_call(
        functools.partial(solve_kernel, axes, n),
        out_shape=[
            jax.ShapeDtypeStruct((2 * split, 2 * split), jnp.bfloat16),
            jax.ShapeDtypeStruct((steps, split), f32),
        ],
        in_specs=[vmem, pl.BlockSpec(memory_space=pl.ANY)],
        out_specs=[vmem, vmem],
        scratch_shapes=[
            chunk_shape,
            own_shape,
            chunk_shape,
            chunk_shape,
            chunk_shape,
            own_shape,
            chunk_shape,
            pltpu.VMEM((2 * split, split), f32),
            pltpu.VMEM((chunks, rows_dev // chunks, cols), f32),
            pltpu.VMEM((split, cols), f32),
            pltpu.VMEM((8, split), f32),
        ]
        + [pltpu.SemaphoreType.DMA((n,))] * 4
        + [pltpu.SemaphoreType.DMA((chunks,))],
        compiler_params=pltpu.CompilerParams(collective_id=0, has_side_effects=True),
        name="solve",
    )(part, modes)
    tile = 2048 if rows_dev % 2048 == 0 else rows_dev
    residual = pl.pallas_call(
        residual_kernel,
        grid=(rows_dev // tile,),
        out_shape=jax.ShapeDtypeStruct((rows_dev, split), f32),
        in_specs=[
            pl.BlockSpec((tile, cols), lambda i: (i, 0)),
            pl.BlockSpec((2 * split, 2 * split), lambda i: (0, 0)),
        ],
        out_specs=pl.BlockSpec((tile, split), lambda i: (i, 0)),
        name="residual",
    )(modes, wide)
    return residual, norms


def solution(mesh):
    axes = tuple((name, mesh.shape[name]) for name in ("rows", "grp"))
    return jax.shard_map(
        functools.partial(on_device, axes),
        mesh=mesh,
        in_specs=(P(("rows", "grp"), None), P()),
        out_specs=(P(("rows", "grp"), None), P()),
        check_vma=False,
    )
```

time: 55.9 us -> 50.4 us (0.902)
  Pallas kernels: 53.7 us -> 48.9 us
  local copies, waits for them, and re-layouts: 1.23 us -> 0.58 us
    pallas_call x2 -> x1, Pallas kernels: 20.5 us -> 9.37 us  [on_device(): pl.pallas_call(residual_kernel, grid=(rows_dev // tile,), out_shape=jax.S...]
    pallas_call x1, Pallas kernels: 27.3 us -> 33.7 us  [on_device(): pl.pallas_call(functools.partial(solve_kernel, axes, n), out_shape=[jax.S...]
    unnamed x1 -> x3, local copies, waits for them, and re-layouts: 1.23 us -> 0.58 us
where the time goes in v3:
time: 50.4 us; the launch traced here: 50.1 us
  Pallas kernels  48.9 us (97%)
  between operations  0.65 us (1%)
  local copies, waits for them, and re-layouts  0.58 us (1%)
    pallas_call x1, Pallas kernels, on_device(): pl.pallas_call(functools.partial(solve_kernel, axes, n), out_shape=[jax.S...  33.7 us
    pallas_call x1, Pallas kernels, on_device(): pl.pallas_call(residual_kernel, grid=(rows_dev // tile,), out_shape=jax.S...  9.37 us
    pallas_call x1, Pallas kernels, on_device(): pl.pallas_call(functools.partial(pick_kernel, axes, n), out_shape=jax.Sha...  5.85 us

profile of v3, /device:TPU:0, one launch (start us, length us, event | category | flops | bytes accessed | tf_op | source)
XLA Modules:
  0.0 50.1 jit_solution(16589880349834427036)
XLA Ops:
  0.6 5.9 %pick.1.part_ref = f32[32,9,128]{2,1,0:T(8,128)} custom-call(s32[196]{0:T(256)} %points_ref.1, f32[12288,256]{1,0:T(8,128)} %modes_ref.5), custom_call_target="tpu_custom_call" | custom-call | tf_op jit(solution)/shard_map/pick/pallas_call | solution.py:324
  6.5 33.7 %solve.1 = (bf16[256,256]{1,0:T(8,128)(2,1)}, f32[4,128]{1,0:T(4,128)}) custom-call(f32[32,9,128]{2,1,0:T(8,128)} %pick.1.part_ref, f32[12288,256]{1,0:T(8,128)} %modes_ref.5), custom_call_target="tpu_custom_call" | custom-call | tf_op jit(solution)/shard_map/solve/pallas_call | solution.py:335
  40.2 0.0 copy-start
  40.2 9.4 %residual.1 = f32[12288,128]{1,0:T(8,128)} custom-call(f32[12288,256]{1,0:T(8,128)} %modes_ref.5, bf16[256,256]{1,0:T(8,128)(2,1)} %get-tuple-element.4.wide_ref), custom_call_target="tpu_custom_call" | custom-call | tf_op jit(solution)/shard_map/residual/pallas_call | solution.py:362
  49.6 0.0 copy-done
  49.6 0.6 %copy.5 = f32[4,128]{1,0:T(4,128)} copy(f32[4,128]{1,0:T(4,128)S(1)} %copy-done) | data formatting | bytes 4096
Async XLA Ops:
  40.2 9.4 %copy-start = (f32[4,128]{1,0:T(4,128)S(1)}, f32[4,128]{1,0:T(4,128)}, u32[]{:S(2)}) copy-start(f32[4,128]{1,0:T(4,128)} %get-tuple-element.9) | copy-start | bytes 6148

commit v4 on v3

--- a/solution.py
+++ b/solution.py
@@ -10,7 +10,7 @@
 PRIOR = 192
 BLOCK = 8
 HOOK_AT = 80
-FIRST, SECOND = 4, 8
+EARLY, FIRST = 2, 6
 HIGH = lax.Precision.HIGHEST
 MESH = pl.DeviceIdType.MESH
 
@@ -62,8 +62,8 @@
 
         return count
 
-    lax.fori_loop(0, npts, issue, 0)
-    lax.fori_loop(0, npts, drain, 0)
+    lax.fori_loop(0, npts, issue, 0, unroll=4)
+    lax.fori_loop(0, npts, drain, 0, unroll=4)
     block = picked[...]
     index = lax.broadcasted_iota(jnp.int32, block.shape, 0)
     chosen = jnp.where(index <= PRIOR, block, 0.0)
@@ -243,10 +243,11 @@
             square[i * rp : (i + 1) * rp, :] = whole[i, 0:rp, :]
         return square[0:split, :], square[split : 2 * split, :]
 
-    first, second = min(FIRST, chunks), min(SECOND, chunks)
+    early, first = min(EARLY, chunks), min(FIRST, chunks)
+    loop(grams, 0, early)
     pl.semaphore_wait(barrier, n - 1)
     loop(lambda off: scatter(part_ref, landed, off).start())
-    loop(grams, 0, first)
+    loop(grams, early, first)
     reduced(part_ref, landed, mine, full)
     loop(grams, first, chunks)
     part2[...] = jnp.zeros_like(part2)
@@ -300,15 +301,29 @@
     return hi, (value - hi.astype(jnp.float32)).astype(jnp.bfloat16)
 
 
-def residual_kernel(modes_ref, wide_ref, res_ref):
-    rows, split = res_ref.shape
-    chunk = 256 if rows % 256 == 0 else rows
+def residual_kernel(modes_ref, wide_ref, res_ref, held, made_buf, read, wrote):
+    chunks, rows, split = made_buf.shape
+    piece = 256 if rows % 256 == 0 else rows
+
+    def fetch(c):
+        return pltpu.make_async_copy(modes_ref.at[pl.ds(c * rows, rows), :], held.at[c], read.at[c])
+
+    def flush(c):
+        return pltpu.make_async_copy(made_buf.at[c], res_ref.at[pl.ds(c * rows, rows), :], wrote.at[c])
+
+    for c in range(chunks):
+        fetch(c).start()
     wide = wide_ref[...]
-    for at in range(0, rows, chunk):
-        hi, lo = halves(modes_ref[at : at + chunk, :split])
-        pair = jnp.concatenate([hi, lo], axis=1)
-        made = jnp.dot(pair, wide, preferred_element_type=jnp.float32)
-        res_ref[at : at + chunk, :] = modes_ref[at : at + chunk, split:] - (made[:, :split] + made[:, split:])
+    for c in range(chunks):
+        fetch(c).wait()
+        for at in range(0, rows, piece):
+            hi, lo = halves(held[c, at : at + piece, :split])
+            pair = jnp.concatenate([hi, lo], axis=1)
+            made = jnp.dot(pair, wide, preferred_element_type=jnp.float32)
+            made_buf[c, at : at + piece, :] = held[c, at : at + piece, split:] - (made[:, :split] + made[:, split:])
+        flush(c).start()
+    for c in range(chunks):
+        flush(c).wait()
 
 
 def on_device(axes, modes, points):
@@ -358,16 +373,18 @@
         compiler_params=pltpu.CompilerParams(collective_id=0, has_side_effects=True),
         name="solve",
     )(part, modes)
-    tile = 2048 if rows_dev % 2048 == 0 else rows_dev
+    any_space = pl.BlockSpec(memory_space=pl.ANY)
     residual = pl.pallas_call(
         residual_kernel,
-        grid=(rows_dev // tile,),
         out_shape=jax.ShapeDtypeStruct((rows_dev, split), f32),
-        in_specs=[
-            pl.BlockSpec((tile, cols), lambda i: (i, 0)),
-            pl.BlockSpec((2 * split, 2 * split), lambda i: (0, 0)),
+        in_specs=[any_space, vmem],
+        out_specs=any_space,
+        scratch_shapes=[
+            pltpu.VMEM((chunks, rows_dev // chunks, cols), f32),
+            pltpu.VMEM((chunks, rows_dev // chunks, split), f32),
+            pltpu.SemaphoreType.DMA((chunks,)),
+            pltpu.SemaphoreType.DMA((chunks,)),
         ],
-        out_specs=pl.BlockSpec((tile, split), lambda i: (i, 0)),
         name="residual",
     )(modes, wide)
     return residual, norms

time: 50.4 us -> 47.9 us (0.950)
  Pallas kernels: 48.9 us -> 46.5 us
    pallas_call x1, Pallas kernels: 5.85 us -> 4.64 us  [on_device(): pl.pallas_call(functools.partial(pick_kernel, axes, n), out_shape=jax.Sha...]
    pallas_call x1, Pallas kernels: 9.37 us -> 8.52 us  [on_device(): pl.pallas_call(residual_kernel, out_shape=jax.ShapeDtypeStruct((rows_dev,...]
where the time goes in v4:
time: 47.9 us; the launch traced here: 47.7 us
  Pallas kernels  46.5 us (97%)
  between operations  0.67 us (1%)
  local copies, waits for them, and re-layouts  0.58 us (1%)
    pallas_call x1, Pallas kernels, on_device(): pl.pallas_call(functools.partial(solve_kernel, axes, n), out_shape=[jax.S...  33.3 us
    pallas_call x1, Pallas kernels, on_device(): pl.pallas_call(residual_kernel, out_shape=jax.ShapeDtypeStruct((rows_dev,...  8.52 us
    pallas_call x1, Pallas kernels, on_device(): pl.pallas_call(functools.partial(pick_kernel, axes, n), out_shape=jax.Sha...  4.64 us

profile of v4, /device:TPU:0, one launch (start us, length us, event | category | flops | bytes accessed | tf_op | source)
XLA Modules:
  0.0 47.7 jit_solution(6625260104045066040)
XLA Ops:
  0.6 4.6 %pick.1.part_ref = f32[32,9,128]{2,1,0:T(8,128)} custom-call(s32[196]{0:T(256)} %points_ref.1, f32[12288,256]{1,0:T(8,128)} %modes_ref.5), custom_call_target="tpu_custom_call" | custom-call | tf_op jit(solution)/shard_map/pick/pallas_call | solution.py:339
  5.3 33.3 %solve.1 = (bf16[256,256]{1,0:T(8,128)(2,1)}, f32[4,128]{1,0:T(4,128)}) custom-call(f32[32,9,128]{2,1,0:T(8,128)} %pick.1.part_ref, f32[12288,256]{1,0:T(8,128)} %modes_ref.5), custom_call_target="tpu_custom_call" | custom-call | tf_op jit(solution)/shard_map/solve/pallas_call | solution.py:350
  38.6 0.0 copy-start
  38.6 8.5 %residual.1 = f32[12288,128]{1,0:T(8,128)} custom-call(f32[12288,256]{1,0:T(8,128)} %modes_ref.5, bf16[256,256]{1,0:T(8,128)(2,1)} %get-tuple-element.4.wide_ref), custom_call_target="tpu_custom_call" | custom-call | tf_op jit(solution)/shard_map/residual/pallas_call | solution.py:377
  47.1 0.0 copy-done
  47.1 0.6 %copy.5 = f32[4,128]{1,0:T(4,128)} copy(f32[4,128]{1,0:T(4,128)S(1)} %copy-done) | data formatting | bytes 4096
Async XLA Ops:
  38.6 8.5 %copy-start = (f32[4,128]{1,0:T(4,128)S(1)}, f32[4,128]{1,0:T(4,128)}, u32[]{:S(2)}) copy-start(f32[4,128]{1,0:T(4,128)} %get-tuple-element.9) | copy-start | bytes 6148
